TPU v7x, 32 devices: a whole 2x2x4 slice. The times are simulated.
32 devices in a mesh: row: 4 (over y, x), col: 8 (over z, core).
Axes of the slice: x: 2, y: 2, z: 4, core: 2. Of those that a mesh axis runs over, the one named last changes fastest.
Arguments:
- left_matrix: float32 [4096, 4096], P('row', 'col'), may hold values from -6 to 6
- right_matrix: float32 [4096, 4096], P('row', 'col'), may hold values from -0.09375 to 0.09375
Outputs:
- product_matrix: float32 [4096, 4096], P('row', 'col')
All inputs are finite; a program needn't handle non-finite values.
Results may differ from a plain program's by a relative error of at most 0.00019.
Values sent between devices are 32-bit elements; how exact they have to be, the bound alone decides.
A program may use at most 64 MiB of HBM per device.

v0:
```python
import functools

import jax
import jax.numpy as jnp
from jax import lax
from jax.experimental import pallas as pl
from jax.experimental.pallas import tpu as pltpu
from jax.sharding import PartitionSpec as P

MESH = pl.DeviceIdType.MESH
CHUNKS = 4


def split(value):
    high = value.astype(jnp.bfloat16)
    low = (value - high.astype(jnp.float32)).astype(jnp.bfloat16)
    return high, low


def kernel(rows, cols, a_in, b_in, out, a_all, b_all, b_high, b_low,
           a_recv, a_send, b_recv, b_send, local):
    row = lax.axis_index("row")
    col = lax.axis_index("col")
    core = lax.rem(col, 2)
    chip = lax.div(col, 2)
    chips = cols // 2
    height, a_depth = a_in.shape
    b_depth = b_in.shape[0]
    per_b = b_depth // a_depth
    size = height // CHUNKS
    partner = chip * 2 + 1 - core

    def left_valid(distance):
        return chip >= distance

    def right_valid(distance):
        return chip + distance < chips

    def a_copy(kind, block, chunk, own):
        part = pl.ds(chunk * size, size)
        target = (col + 2, col - 2, partner)[kind]
        return pltpu.make_async_remote_copy(
            src_ref=a_in.at[part] if own else a_all.at[block, part],
            dst_ref=a_all.at[block, part],
            send_sem=a_send.at[kind, block, chunk],
            recv_sem=a_recv.at[block, chunk],
            device_id={"col": target}, device_id_type=MESH)

    def a_wait(block, chunk):
        a_copy(2, block, chunk, False).wait_recv()

    def b_copy(peer, source):
        return pltpu.make_async_remote_copy(
            src_ref=b_in, dst_ref=b_all.at[source],
            send_sem=b_send.at[peer], recv_sem=b_recv.at[source],
            device_id={"row": peer}, device_id_type=MESH)

    barrier = pltpu.get_barrier_semaphore()

    @pl.when(chip > 0)
    def _():
        pl.semaphore_signal(barrier, inc=1, device_id={"col": col - 2}, device_id_type=MESH)

    @pl.when(chip < chips - 1)
    def _():
        pl.semaphore_signal(barrier, inc=1, device_id={"col": col + 2}, device_id_type=MESH)

    pl.semaphore_signal(barrier, inc=1, device_id={"col": partner}, device_id_type=MESH)
    peers = [lax.rem(row + offset, rows) for offset in range(1, rows)]
    for peer in peers:
        pl.semaphore_signal(barrier, inc=1, device_id={"row": peer}, device_id_type=MESH)
    own_a = pltpu.make_async_copy(a_in, a_all.at[col], local.at[0])
    own_b = pltpu.make_async_copy(b_in, b_all.at[row], local.at[1])
    own_a.start()
    own_b.start()
    near = jnp.where(chip > 0, 1, 0) + jnp.where(chip < chips - 1, 1, 0)
    pl.semaphore_wait(barrier, rows + near)

    for chunk in range(CHUNKS):
        @pl.when(right_valid(1))
        def _():
            a_copy(0, col, chunk, True).start()

        @pl.when(left_valid(1))
        def _():
            a_copy(1, col, chunk, True).start()
    for peer in peers:
        b_copy(peer, row).start()
    for chunk in range(CHUNKS):
        a_copy(2, col, chunk, True).start()

    out[...] = jnp.zeros_like(out)
    own_a.wait()
    own_b.wait()

    def multiply(block, chunk):
        part = pl.ds(pl.multiple_of(chunk * size, size), size)
        source = lax.div(block, per_b)
        offset = pl.multiple_of(lax.rem(block, per_b) * a_depth, a_depth)
        depth = pl.ds(offset, a_depth)
        high, low = split(a_all[block, part, :])
        right_high = b_high[source, depth, :]
        right_low = b_low[source, depth, :]
        dot = functools.partial(jnp.dot, preferred_element_type=jnp.float32)
        out[part, :] += (dot(low, right_high) + dot(high, right_low)) + dot(high, right_high)

    def split_b(source):
        @pl.loop(0, b_depth // 128)
        def _(index):
            part = pl.ds(pl.multiple_of(index * 128, 128), 128)
            high, low = split(b_all[source, part, :])
            b_high[source, part, :] = high
            b_low[source, part, :] = low

    def multiply_block(block):
        @pl.loop(0, CHUNKS)
        def _(chunk):
            multiply(block, chunk)

    for distance in range(1, chips - 1):
        for chunk in range(CHUNKS):
            @pl.when(left_valid(distance))
            def _():
                block = col - 2 * distance
                a_wait(block, chunk)

                @pl.when(right_valid(1))
                def _():
                    a_copy(0, block, chunk, False).start()
                a_copy(2, block, chunk, False).start()

            @pl.when(right_valid(distance))
            def _():
                block = col + 2 * distance
                a_wait(block, chunk)

                @pl.when(left_valid(1))
                def _():
                    a_copy(1, block, chunk, False).start()
                a_copy(2, block, chunk, False).start()

    split_b(row)
    for peer in peers:
        b_copy(peer, peer).wait_recv()
        split_b(peer)

    for chunk in range(CHUNKS):
        a_wait(partner, chunk)
    multiply_block(col)
    multiply_block(partner)
    for distance in range(1, chips - 1):
        for valid, step in ((left_valid, -2), (right_valid, 2)):
            @pl.when(valid(distance))
            def _():
                for chunk in range(CHUNKS):
                    a_wait(partner + step * distance, chunk)
                multiply_block(col + step * distance)
                multiply_block(partner + step * distance)

    if chips > 1:
        for valid, step in ((left_valid, -2), (right_valid, 2)):
            @pl.when(valid(chips - 1))
            def _():
                block = col + step * (chips - 1)
                other = partner + step * (chips - 1)
                for chunk in range(CHUNKS):
                    a_wait(block, chunk)
                    a_copy(2, block, chunk, False).start()
                    multiply(block, chunk)
                    a_wait(other, chunk)
                    multiply(other, chunk)

    for peer in peers:
        b_copy(peer, row).wait_send()
    for chunk in range(CHUNKS):
        a_copy(2, col, chunk, True).wait_send()
        for distance in range(0, chips):
            @pl.when(left_valid(distance) & right_valid(1))
            def _():
                a_copy(0, col - 2 * distance, chunk, False).wait_send()

            @pl.when(right_valid(distance) & left_valid(1))
            def _():
                a_copy(1, col + 2 * distance, chunk, False).wait_send()
        for distance in range(1, chips):
            @pl.when(left_valid(distance))
            def _():
                a_copy(2, col - 2 * distance, chunk, False).wait_send()

            @pl.when(right_valid(distance))
            def _():
                a_copy(2, col + 2 * distance, chunk, False).wait_send()


def body(rows, cols, left_matrix, right_matrix):
    height, a_depth = left_matrix.shape
    b_depth, width = right_matrix.shape
    return pl.pallas_call(
        functools.partial(kernel, rows, cols),
        out_shape=jax.ShapeDtypeStruct((height, width), jnp.float32),
        in_specs=[pl.BlockSpec(memory_space=pl.ANY)] * 2,
        out_specs=pl.BlockSpec(memory_space=pltpu.VMEM),
        scratch_shapes=[
            pltpu.VMEM((cols, height, a_depth), jnp.float32),
            pltpu.VMEM((rows, b_depth, width), jnp.float32),
            pltpu.VMEM((rows, b_depth, width), jnp.bfloat16),
            pltpu.VMEM((rows, b_depth, width), jnp.bfloat16),
            pltpu.SemaphoreType.DMA((cols, CHUNKS)),
            pltpu.SemaphoreType.DMA((3, cols, CHUNKS)),
            pltpu.SemaphoreType.DMA((rows,)),
            pltpu.SemaphoreType.DMA((rows,)),
            pltpu.SemaphoreType.DMA((2,)),
        ],
        compiler_params=pltpu.CompilerParams(
            collective_id=0, has_side_effects=True, vmem_limit_bytes=56 * 2**20),
    )(left_matrix, right_matrix)


STEPS = 8
LAG = 2
EARLY = 2


def shared_kernel(a_in, b_in, out, a_all, b_all, b_high, b_low, c_all, c_high, c_low, partial,
                  a_recv, a_send, b_recv, b_send, c_recv, c_send, p_recv, p_send, local):
    row = lax.axis_index("row")
    col = lax.axis_index("col")
    core = lax.rem(col, 2)
    chip = lax.div(col, 2)
    partner = chip * 2 + 1 - core
    side = lax.div(chip, 2)
    y = lax.div(row, 2)
    x = lax.rem(row, 2)
    x_near = y * 2 + 1 - x
    y_near = (1 - y) * 2 + x
    far_corner = (1 - y) * 2 + 1 - x
    other_side = 1 - side
    end = 6 * side + core
    middle = 2 + 2 * side + core
    other_middle = 4 - 2 * side + core
    other_end = 6 - 6 * side + core
    swap = 1 - 2 * core
    is_end = (chip == 0) | (chip == 3)
    is_middle = (chip == 1) | (chip == 2)
    height, a_depth = a_in.shape
    b_depth = b_in.shape[0]
    a_size = height // STEPS
    b_size = b_depth // STEPS

    def a_copy(kind, target, block, step, own=False):
        part = pl.ds(step * a_size, a_size)
        return pltpu.make_async_remote_copy(
            src_ref=a_in.at[part] if own else a_all.at[block, part],
            dst_ref=a_all.at[block, part],
            send_sem=a_send.at[kind, block, step], recv_sem=a_recv.at[block, step],
            device_id={"col": target}, device_id_type=MESH)

    def a_wait(block, step):
        a_copy(2, partner, block, step).wait_recv()

    def b_copy(kind, target, source, step, own=False):
        part = pl.ds(step * b_size, b_size)
        return pltpu.make_async_remote_copy(
            src_ref=b_in.at[part] if own else b_all.at[source, part],
            dst_ref=b_all.at[source, part],
            send_sem=b_send.at[kind, step], recv_sem=b_recv.at[source, step],
            device_id={"row": target}, device_id_type=MESH)

    def b_wait(source):
        for step in range(STEPS):
            b_copy(0, x_near, source, step).wait_recv()

    def c_down(step, own):
        part = pl.ds(step * b_size, b_size)
        return pltpu.make_async_remote_copy(
            src_ref=b_in.at[part] if own else b_all.at[y_near, part],
            dst_ref=c_all.at[x, part],
            send_sem=c_send.at[0, step], recv_sem=c_recv.at[x, step],
            device_id={"col": middle}, device_id_type=MESH)

    def c_across(slot, step):
        part = pl.ds(step * b_size, b_size)
        return pltpu.make_async_remote_copy(
            src_ref=c_all.at[slot, part], dst_ref=c_all.at[slot, part],
            send_sem=c_send.at[1, step], recv_sem=c_recv.at[slot, step],
            device_id={"row": x_near}, device_id_type=MESH)

    def p_copy(step):
        part = pl.ds(step * a_size, a_size)
        return pltpu.make_async_remote_copy(
            src_ref=partial.at[part], dst_ref=partial.at[part],
            send_sem=p_send.at[step], recv_sem=p_recv.at[step],
            device_id={"col": end}, device_id_type=MESH)

    def split_into(source, full, high_all, low_all):
        @pl.loop(0, b_depth // 128)
        def _(index):
            part = pl.ds(pl.multiple_of(index * 128, 128), 128)
            high, low = split(full[source, part, :])
            high_all[source, part, :] = high
            low_all[source, part, :] = low

    dot = functools.partial(jnp.dot, preferred_element_type=jnp.float32)

    def multiply(into, part, block, high_all, low_all, source, half):
        depth = pl.ds(pl.multiple_of(half * a_depth, a_depth), a_depth)
        high, low = split(a_all[block, part, :])
        right_high = high_all[source, depth, :]
        right_low = low_all[source, depth, :]
        into[part, :] += (dot(low, right_high) + dot(high, right_low)) + dot(high, right_high)

    def multiply_source(source):
        @pl.loop(0, 8)
        def _(index):
            size = height // 4
            part = pl.ds(pl.multiple_of(lax.rem(index, 4) * size, size), size)
            half = lax.div(index, 4)
            multiply(out, part, 2 * source + half, b_high, b_low, source, half)

    barrier = pltpu.get_barrier_semaphore()

    def greet(target):
        pl.semaphore_signal(barrier, inc=1, device_id=target, device_id_type=MESH)

    greet({"col": partner})
    for peer in (x_near, y_near, far_corner):
        greet({"row": peer})

    @pl.when(is_end)
    def _():
        greet({"col": middle})

    @pl.when(is_middle)
    def _():
        greet({"col": end})
        greet({"col": other_middle})

    own_a = pltpu.make_async_copy(a_in, a_all.at[col], local.at[0])
    own_b = pltpu.make_async_copy(b_in, b_all.at[row], local.at[1])
    own_a.start()
    own_b.start()
    pl.semaphore_wait(barrier, jnp.where(is_end, 5, 6))

    @pl.when(is_end)
    def _():
        donor = y == other_side
        keeper = y == side

        @pl.when(donor)
        def _():
            for step in range(STEPS):
                c_down(step, True).start()
                b_copy(1, y_near, row, step, True).start()

        @pl.when(keeper)
        def _():
            for step in range(STEPS):
                b_copy(0, x_near, row, step, True).start()
                b_copy(1, y_near, row, step, True).start()
            for step in range(STEPS):
                b_copy(2, far_corner, row, step, True).start()

        for step in range(STEPS):
            a_copy(2, partner, col, step, True).start()
        out[...] = jnp.zeros_like(out)
        own_a.wait()
        own_b.wait()

        @pl.when(keeper)
        def _():
            for step in range(STEPS):
                b_copy(1, y_near, y_near, step).wait_recv()
                c_down(step, False).start()

        for step in range(STEPS):
            a_copy(0, middle, col, step, True).start()
        for step in range(STEPS):
            a_wait(middle, step)
            a_copy(2, partner, middle, step).start()

        @pl.when(donor)
        def _():
            b_wait(y_near)
            b_wait(far_corner)

        @pl.when(keeper)
        def _():
            b_wait(x_near)

        for step in range(STEPS):
            a_wait(end + swap, step)
            a_wait(middle + swap, step)
        for index in range(2):
            split_into(2 * side + index, b_all, b_high, b_low)
            multiply_source(2 * side + index)
        for step in range(STEPS):
            part = pl.ds(step * a_size, a_size)
            p_copy(step).wait_recv()
            out[part, :] += partial[part, :]

        @pl.when(donor)
        def _():
            for step in range(STEPS):
                c_down(step, True).wait_send()
                b_copy(1, y_near, row, step, True).wait_send()

        @pl.when(keeper)
        def _():
            for step in range(STEPS):
                for kind, peer in enumerate((x_near, y_near, far_corner)):
                    b_copy(kind, peer, row, step, True).wait_send()
                c_down(step, False).wait_send()
        for step in range(STEPS):
            a_copy(2, partner, col, step, True).wait_send()
            a_copy(0, middle, col, step, True).wait_send()
            a_copy(2, partner, middle, step).wait_send()

    @pl.when(is_middle)
    def _():
        sent = []

        def go(copy):
            copy.start()
            sent.append(copy)

        for step in range(STEPS):
            go(a_copy(1, end, col, step, True))
            go(a_copy(0, other_middle, col, step, True))
        for step in range(EARLY):
            go(b_copy(0, x_near, row, step, True))
        for step in range(STEPS):
            go(b_copy(1, y_near, row, step, True))
        for step in range(STEPS):
            go(a_copy(2, partner, col, step, True))
        out[...] = jnp.zeros_like(out)
        partial[...] = jnp.zeros_like(partial)
        own_a.wait()
        own_b.wait()
        split_into(row, b_all, b_high, b_low)

        for step in range(STEPS):
            c_across(x, step).wait_recv()
            go(c_across(x, step))
            a_wait(other_middle, step)
            go(a_copy(2, partner, other_middle, step))
        for step in range(EARLY, STEPS):
            go(b_copy(0, x_near, row, step, True))
        split_into(x, c_all, c_high, c_low)

        for step in range(STEPS + LAG):
            if step < STEPS:
                a_wait(end, step)
                go(a_copy(0, other_middle, end, step))
                go(a_copy(2, partner, end, step))
            if step < LAG:
                continue
            if step == LAG:
                b_wait(y_near)
                split_into(y_near, b_all, b_high, b_low)
                for index in range(STEPS):
                    c_across(1 - x, index).wait_recv()
                split_into(1 - x, c_all, c_high, c_low)
            late = step - LAG
            part = pl.ds(late * a_size, a_size)
            a_wait(other_end, late)
            go(a_copy(2, partner, other_end, late))
            for block in (middle, other_middle, end, other_end):
                a_wait(block + swap, late)

            @pl.loop(0, 4)
            def _(index):
                multiply(partial, part, 4 * other_side + index, c_high, c_low,
                         lax.div(index, 2), lax.rem(index, 2))

            @pl.loop(0, 4)
            def _(index):
                source = lax.div(index, 2) * 2 + x
                half = lax.rem(index, 2)
                multiply(out, part, 2 * source + half, b_high, b_low, source, half)

            go(p_copy(late))
            b_copy(0, x_near, x_near, late).wait_recv()
            go(b_copy(2, y_near, x_near, late))

        split_into(x_near, b_all, b_high, b_low)
        multiply_source(x_near)
        b_wait(far_corner)
        split_into(far_corner, b_all, b_high, b_low)
        multiply_source(far_corner)
        for copy in sent:
            copy.wait_send()


def shared_body(left_matrix, right_matrix):
    height, a_depth = left_matrix.shape
    b_depth, width = right_matrix.shape
    dma = pltpu.SemaphoreType.DMA
    return pl.pallas_call(
        shared_kernel,
        out_shape=jax.ShapeDtypeStruct((height, width), jnp.float32),
        in_specs=[pl.BlockSpec(memory_space=pl.ANY)] * 2,
        out_specs=pl.BlockSpec(memory_space=pltpu.VMEM),
        scratch_shapes=[
            pltpu.VMEM((8, height, a_depth), jnp.float32),
            pltpu.VMEM((4, b_depth, width), jnp.float32),
            pltpu.VMEM((4, b_depth, width), jnp.bfloat16),
            pltpu.VMEM((4, b_depth, width), jnp.bfloat16),
            pltpu.VMEM((2, b_depth, width), jnp.float32),
            pltpu.VMEM((2, b_depth, width), jnp.bfloat16),
            pltpu.VMEM((2, b_depth, width), jnp.bfloat16),
            pltpu.VMEM((height, width), jnp.float32),
            dma((8, STEPS)), dma((3, 8, STEPS)), dma((4, STEPS)), dma((3, STEPS)),
            dma((2, STEPS)), dma((2, STEPS)), dma((STEPS,)), dma((STEPS,)), dma((2,)),
        ],
        compiler_params=pltpu.CompilerParams(
            collective_id=1, has_side_effects=True, vmem_limit_bytes=60 * 2**20),
    )(left_matrix, right_matrix)


def solution(mesh):
    placed = (P("row", "col"), P("row", "col"))
    rows, cols = mesh.shape["row"], mesh.shape["col"]
    part = shared_body if (rows, cols) == (4, 8) else functools.partial(body, rows, cols)
    return jax.shard_map(
        part, mesh=mesh, in_specs=placed, out_specs=P("row", "col"), check_vma=False
    )
```

profile of v0, /device:TPU:17, one launch (start us, length us, event | category | flops | bytes accessed | tf_op | source)
XLA Modules:
  0.0 139.4 jit_solution(9703523511718182000)
XLA Ops:
  0.0 136.3 %shard_map.28 = f32[1024,512]{1,0:T(8,128)} custom-call(f32[1024,512]{1,0:T(8,128)} %a_in.1, f32[1024,512]{1,0:T(8,128)} %b_in.1), custom_call_target="tpu_custom_call" | custom-call | tf_op jit(solution)/shard_map/pallas_call | solution.py:498
  136.3 3.1 %copy.4 = f32[1024,512]{1,0:T(8,128)} copy(f32[1024,512]{1,0:T(8,128)} %shard_map.28) | data formatting | bytes 4194304
where the time goes:
time: 140 us; the launch traced here: 139 us
  Pallas kernels  136 us (97%)
  local copies, waits for them, and re-layouts  3.08 us (2%)
    pallas_call x1, Pallas kernels, shared_body(): pl.pallas_call(shared_kernel, out_shape=jax.ShapeDtypeStruct((height, wid...  136 us
    unnamed x1, local copies, waits for them, and re-layouts  3.08 us

commit v1 on v0

--- a/solution.py
+++ b/solution.py
@@ -216,9 +216,15 @@
     )(left_matrix, right_matrix)
 
 
-STEPS = 8
-LAG = 2
-EARLY = 2
+STEPS = 16
+FINE = 32
+HEAD = 4
+PRE = 1
+GROUPS = 4
+END_AT = 13
+FAR_AT = 16
+SUM_AT = 17
+LANDED_AT = 20
 
 
 def shared_kernel(a_in, b_in, out, a_all, b_all, b_high, b_low, c_all, c_high, c_low, partial,
@@ -242,80 +248,87 @@
     swap = 1 - 2 * core
     is_end = (chip == 0) | (chip == 3)
     is_middle = (chip == 1) | (chip == 2)
+    keeper = y == side
+    donor = y == other_side
     height, a_depth = a_in.shape
     b_depth = b_in.shape[0]
     a_size = height // STEPS
-    b_size = b_depth // STEPS
+    b_size = b_depth // FINE
+    group = height // GROUPS
+
+    def rows_of(index, size):
+        return pl.ds(pl.multiple_of(index * size, size), size)
+
+    def remote(source, target, send, recv, device):
+        return pltpu.make_async_remote_copy(
+            src_ref=source, dst_ref=target, send_sem=send, recv_sem=recv,
+            device_id=device, device_id_type=MESH)
 
     def a_copy(kind, target, block, step, own=False):
-        part = pl.ds(step * a_size, a_size)
-        return pltpu.make_async_remote_copy(
-            src_ref=a_in.at[part] if own else a_all.at[block, part],
-            dst_ref=a_all.at[block, part],
-            send_sem=a_send.at[kind, block, step], recv_sem=a_recv.at[block, step],
-            device_id={"col": target}, device_id_type=MESH)
+        part = rows_of(step, a_size)
+        return remote(a_in.at[part] if own else a_all.at[block, part], a_all.at[block, part],
+                      a_send.at[kind, block], a_recv.at[block, step], {"col": target})
 
     def a_wait(block, step):
         a_copy(2, partner, block, step).wait_recv()
 
-    def b_copy(kind, target, source, step, own=False):
-        part = pl.ds(step * b_size, b_size)
-        return pltpu.make_async_remote_copy(
-            src_ref=b_in.at[part] if own else b_all.at[source, part],
-            dst_ref=b_all.at[source, part],
-            send_sem=b_send.at[kind, step], recv_sem=b_recv.at[source, step],
-            device_id={"row": target}, device_id_type=MESH)
-
-    def b_wait(source):
-        for step in range(STEPS):
-            b_copy(0, x_near, source, step).wait_recv()
-
-    def c_down(step, own):
-        part = pl.ds(step * b_size, b_size)
-        return pltpu.make_async_remote_copy(
-            src_ref=b_in.at[part] if own else b_all.at[y_near, part],
-            dst_ref=c_all.at[x, part],
-            send_sem=c_send.at[0, step], recv_sem=c_recv.at[x, step],
-            device_id={"col": middle}, device_id_type=MESH)
-
-    def c_across(slot, step):
-        part = pl.ds(step * b_size, b_size)
-        return pltpu.make_async_remote_copy(
-            src_ref=c_all.at[slot, part], dst_ref=c_all.at[slot, part],
-            send_sem=c_send.at[1, step], recv_sem=c_recv.at[slot, step],
-            device_id={"row": x_near}, device_id_type=MESH)
+    def a_sent(kind, block):
+        remote(a_all.at[block], a_all.at[block], a_send.at[kind, block], a_recv.at[block, 0],
+               {"col": partner}).wait_send()
+
+    def b_copy(kind, source, step, own=False):
+        part = rows_of(step, b_size)
+        return remote(b_in.at[part] if own else b_all.at[source, part], b_all.at[source, part],
+                      b_send.at[kind, source], b_recv.at[source, step],
+                      {"row": (x_near, y_near)[kind]})
+
+    def b_wait(source, first, last):
+        @pl.loop(first, last)
+        def _(step):
+            b_copy(0, source, step).wait_recv()
+
+    def b_sent(kind, source, size):
+        part = pl.ds(0, size)
+        remote(b_all.at[source, part], b_all.at[source, part], b_send.at[kind, source],
+               b_recv.at[source, 0], {"row": x_near}).wait_send()
+
+    def c_copy(kind, slot, step, own=False):
+        part = rows_of(step, b_size)
+        target = ({"col": middle}, {"row": far_corner}, {"row": x_near}, {"row": y_near})[kind]
+        return remote(b_in.at[part] if own else c_all.at[slot, part], c_all.at[slot, part],
+                      c_send.at[kind], c_recv.at[slot, step], target)
+
+    def c_sent(kind, size):
+        part = pl.ds(0, size)
+        remote(c_all.at[0, part], c_all.at[0, part], c_send.at[kind], c_recv.at[0, 0],
+               {"row": x_near}).wait_send()
 
     def p_copy(step):
-        part = pl.ds(step * a_size, a_size)
-        return pltpu.make_async_remote_copy(
-            src_ref=partial.at[part], dst_ref=partial.at[part],
-            send_sem=p_send.at[step], recv_sem=p_recv.at[step],
-            device_id={"col": end}, device_id_type=MESH)
-
-    def split_into(source, full, high_all, low_all):
-        @pl.loop(0, b_depth // 128)
+        part = rows_of(step, a_size)
+        return remote(partial.at[part], partial.at[part], p_send, p_recv.at[step], {"col": end})
+
+    def split_rows(source, part, full, high_all, low_all):
+        high, low = split(full[source, part, :])
+        high_all[source, part, :] = high
+        low_all[source, part, :] = low
+
+    def split_b(source, first, last):
+        @pl.loop(first, last)
         def _(index):
-            part = pl.ds(pl.multiple_of(index * 128, 128), 128)
-            high, low = split(full[source, part, :])
-            high_all[source, part, :] = high
-            low_all[source, part, :] = low
+            split_rows(source, rows_of(index, 128), b_all, b_high, b_low)
 
     dot = functools.partial(jnp.dot, preferred_element_type=jnp.float32)
 
-    def multiply(into, part, block, high_all, low_all, source, half):
-        depth = pl.ds(pl.multiple_of(half * a_depth, a_depth), a_depth)
+    def term(part, block, high_all, low_all, source, half):
+        depth = rows_of(half, a_depth)
         high, low = split(a_all[block, part, :])
         right_high = high_all[source, depth, :]
         right_low = low_all[source, depth, :]
-        into[part, :] += (dot(low, right_high) + dot(high, right_low)) + dot(high, right_high)
-
-    def multiply_source(source):
-        @pl.loop(0, 8)
-        def _(index):
-            size = height // 4
-            part = pl.ds(pl.multiple_of(lax.rem(index, 4) * size, size), size)
-            half = lax.div(index, 4)
-            multiply(out, part, 2 * source + half, b_high, b_low, source, half)
+        return (dot(low, right_high) + dot(high, right_low)) + dot(high, right_high)
+
+    def job(source, half, index):
+        part = rows_of(index, group)
+        out[part, :] += term(part, 2 * source + half, b_high, b_low, source, half)
 
     barrier = pltpu.get_barrier_semaphore()
 
@@ -323,12 +336,13 @@
         pl.semaphore_signal(barrier, inc=1, device_id=target, device_id_type=MESH)
 
     greet({"col": partner})
-    for peer in (x_near, y_near, far_corner):
-        greet({"row": peer})
+    greet({"row": x_near})
+    greet({"row": y_near})
 
     @pl.when(is_end)
     def _():
         greet({"col": middle})
+        greet({"row": far_corner})
 
     @pl.when(is_middle)
     def _():
@@ -339,156 +353,295 @@
     own_b = pltpu.make_async_copy(b_in, b_all.at[row], local.at[1])
     own_a.start()
     own_b.start()
-    pl.semaphore_wait(barrier, jnp.where(is_end, 5, 6))
+    pl.semaphore_wait(barrier, 5)
 
     @pl.when(is_end)
     def _():
-        donor = y == other_side
-        keeper = y == side
+        first = 2 * side + x
+        second = 2 * side + 1 - x
+
+        for step in range(PRE):
+            a_copy(0, middle, col, step, True).start()
 
         @pl.when(donor)
         def _():
-            for step in range(STEPS):
-                c_down(step, True).start()
-                b_copy(1, y_near, row, step, True).start()
+            @pl.loop(0, FINE)
+            def _(step):
+                c_copy(1, x, step, True).start()
+                c_copy(0, x, step, True).start()
+
+            @pl.loop(PRE, STEPS)
+            def _(step):
+                a_copy(0, middle, col, step, True).start()
 
         @pl.when(keeper)
         def _():
-            for step in range(STEPS):
-                b_copy(0, x_near, row, step, True).start()
-                b_copy(1, y_near, row, step, True).start()
-            for step in range(STEPS):
-                b_copy(2, far_corner, row, step, True).start()
-
-        for step in range(STEPS):
+            @pl.loop(0, FINE)
+            def _(step):
+                b_copy(0, row, step, True).start()
+                b_copy(1, row, step, True).start()
+
+        @pl.loop(0, STEPS)
+        def _(step):
             a_copy(2, partner, col, step, True).start()
         out[...] = jnp.zeros_like(out)
         own_a.wait()
         own_b.wait()
 
+        @pl.loop(0, LANDED_AT + STEPS)
+        def _(t):
+            @pl.when(keeper & (t < STEPS))
+            def _():
+                for index in range(2):
+                    c_copy(0, 1 - x, 2 * t + index).wait_recv()
+                    c_copy(0, 1 - x, 2 * t + index).start()
+
+            @pl.when(keeper & (t == STEPS))
+            def _():
+                @pl.loop(PRE, STEPS)
+                def _(step):
+                    a_copy(0, middle, col, step, True).start()
+                b_wait(x_near, 0, FINE)
+
+            @pl.when(donor & (t < STEPS))
+            def _():
+                for index in range(2):
+                    b_copy(0, y_near, 2 * t + index).wait_recv()
+                    b_copy(0, y_near, 2 * t + index).start()
+
+            @pl.when(t < STEPS)
+            def _():
+                a_wait(middle, t)
+                a_copy(2, partner, middle, t).start()
+                a_wait(end + swap, t)
+
+            @pl.when((t >= 1) & (t < STEPS + 1))
+            def _():
+                a_wait(middle + swap, t - 1)
+
+            @pl.when(t == STEPS + 1)
+            def _():
+                split_b(first, 0, 8)
+
+            @pl.when((t >= STEPS + 2) & (t < STEPS + 10))
+            def _():
+                u = t - STEPS - 2
+                job(first, lax.div(u, GROUPS), lax.rem(u, GROUPS))
+
+            @pl.when(donor & (t == STEPS + 12))
+            def _():
+                b_wait(far_corner, 0, FINE // 2)
+
+            @pl.when(t == STEPS + 12)
+            def _():
+                split_b(second, 0, 4)
+
+            @pl.when((t >= STEPS + 13) & (t < STEPS + 17))
+            def _():
+                job(second, 0, t - STEPS - 13)
+
+            @pl.when(donor & (t == STEPS + 18))
+            def _():
+                b_wait(far_corner, FINE // 2, FINE)
+
+            @pl.when(t == STEPS + 18)
+            def _():
+                split_b(second, 4, 8)
+
+                @pl.loop(0, GROUPS)
+                def _(index):
+                    job(second, 1, index)
+
+            @pl.when(t >= LANDED_AT)
+            def _():
+                part = rows_of(t - LANDED_AT, a_size)
+                p_copy(t - LANDED_AT).wait_recv()
+                out[part, :] += partial[part, :]
+
+        @pl.when(donor)
+        def _():
+            c_sent(0, b_depth)
+            c_sent(1, b_depth)
+            b_sent(0, y_near, b_depth)
+
         @pl.when(keeper)
         def _():
-            for step in range(STEPS):
-                b_copy(1, y_near, y_near, step).wait_recv()
-                c_down(step, False).start()
-
-        for step in range(STEPS):
-            a_copy(0, middle, col, step, True).start()
-        for step in range(STEPS):
-            a_wait(middle, step)
-            a_copy(2, partner, middle, step).start()
-
-        @pl.when(donor)
-        def _():
-            b_wait(y_near)
-            b_wait(far_corner)
-
-        @pl.when(keeper)
-        def _():
-            b_wait(x_near)
-
-        for step in range(STEPS):
-            a_wait(end + swap, step)
-            a_wait(middle + swap, step)
-        for index in range(2):
-            split_into(2 * side + index, b_all, b_high, b_low)
-            multiply_source(2 * side + index)
-        for step in range(STEPS):
-            part = pl.ds(step * a_size, a_size)
-            p_copy(step).wait_recv()
-            out[part, :] += partial[part, :]
-
-        @pl.when(donor)
-        def _():
-            for step in range(STEPS):
-                c_down(step, True).wait_send()
-                b_copy(1, y_near, row, step, True).wait_send()
-
-        @pl.when(keeper)
-        def _():
-            for step in range(STEPS):
-                for kind, peer in enumerate((x_near, y_near, far_corner)):
-                    b_copy(kind, peer, row, step, True).wait_send()
-                c_down(step, False).wait_send()
-        for step in range(STEPS):
-            a_copy(2, partner, col, step, True).wait_send()
-            a_copy(0, middle, col, step, True).wait_send()
-            a_copy(2, partner, middle, step).wait_send()
+            c_sent(0, b_depth)
+            b_sent(0, row, b_depth)
+            b_sent(1, row, b_depth)
+        a_sent(0, col)
+        a_sent(2, col)
+        a_sent(2, middle)
 
     @pl.when(is_middle)
     def _():
-        sent = []
-
-        def go(copy):
-            copy.start()
-            sent.append(copy)
-
-        for step in range(STEPS):
-            go(a_copy(1, end, col, step, True))
-            go(a_copy(0, other_middle, col, step, True))
-        for step in range(EARLY):
-            go(b_copy(0, x_near, row, step, True))
-        for step in range(STEPS):
-            go(b_copy(1, y_near, row, step, True))
-        for step in range(STEPS):
-            go(a_copy(2, partner, col, step, True))
+        inner = (row == 1) | (row == 2)
+        slot = lax.rem(x + jnp.where(keeper, 1, 0), 2)
+
+        @pl.loop(0, STEPS)
+        def _(step):
+            a_copy(0, other_middle, col, step, True).start()
+            a_copy(1, end, col, step, True).start()
+
+            @pl.when(step < HEAD)
+            def _():
+                b_copy(0, row, step, True).start()
+                b_copy(1, row, step, True).start()
+            a_copy(2, partner, col, step, True).start()
         out[...] = jnp.zeros_like(out)
-        partial[...] = jnp.zeros_like(partial)
         own_a.wait()
         own_b.wait()
-        split_into(row, b_all, b_high, b_low)
-
-        for step in range(STEPS):
-            c_across(x, step).wait_recv()
-            go(c_across(x, step))
-            a_wait(other_middle, step)
-            go(a_copy(2, partner, other_middle, step))
-        for step in range(EARLY, STEPS):
-            go(b_copy(0, x_near, row, step, True))
-        split_into(x, c_all, c_high, c_low)
-
-        for step in range(STEPS + LAG):
-            if step < STEPS:
-                a_wait(end, step)
-                go(a_copy(0, other_middle, end, step))
-                go(a_copy(2, partner, end, step))
-            if step < LAG:
-                continue
-            if step == LAG:
-                b_wait(y_near)
-                split_into(y_near, b_all, b_high, b_low)
-                for index in range(STEPS):
-                    c_across(1 - x, index).wait_recv()
-                split_into(1 - x, c_all, c_high, c_low)
-            late = step - LAG
-            part = pl.ds(late * a_size, a_size)
-            a_wait(other_end, late)
-            go(a_copy(2, partner, other_end, late))
-            for block in (middle, other_middle, end, other_end):
-                a_wait(block + swap, late)
-
-            @pl.loop(0, 4)
-            def _(index):
-                multiply(partial, part, 4 * other_side + index, c_high, c_low,
-                         lax.div(index, 2), lax.rem(index, 2))
-
-            @pl.loop(0, 4)
-            def _(index):
-                source = lax.div(index, 2) * 2 + x
-                half = lax.rem(index, 2)
-                multiply(out, part, 2 * source + half, b_high, b_low, source, half)
-
-            go(p_copy(late))
-            b_copy(0, x_near, x_near, late).wait_recv()
-            go(b_copy(2, y_near, x_near, late))
-
-        split_into(x_near, b_all, b_high, b_low)
-        multiply_source(x_near)
-        b_wait(far_corner)
-        split_into(far_corner, b_all, b_high, b_low)
-        multiply_source(far_corner)
-        for copy in sent:
-            copy.wait_send()
+        split_b(row, 0, 8)
+        for step in range(PRE):
+            a_wait(end, step)
+            a_copy(0, other_middle, end, step).start()
+            a_copy(2, partner, end, step).start()
+
+        def sequence(s):
+            late = s >= 28
+            q = jnp.where(s >= 23, s - 14, s - 8)
+            g, w = lax.div(q, 3), lax.rem(q, 3)
+            last = (s >= 17) & (s < 23) | (s == 26) | (s == 27)
+            v = jnp.where(s >= 26, s - 20, s - 17)
+            near = lambda p: jnp.where(p == 0, x_near, y_near)
+            u = lax.rem(s, 8)
+            source = jnp.where(inner, row, near(lax.div(u, GROUPS)))
+            half = jnp.where(inner, lax.div(u, GROUPS), 0)
+            index = lax.rem(u, GROUPS)
+            mid = (s >= 8) & (s < 28)
+            pair = mid & (w < 2)
+            source = jnp.where(mid, jnp.where(w < 2, jnp.where(inner, near(w), row), far_corner), source)
+            half = jnp.where(mid, jnp.where(pair & ~inner, w, 0), half)
+            index = jnp.where(mid, g, index)
+            source = jnp.where(last, near(lax.rem(v, 2)), source)
+            half = jnp.where(last, 1, half)
+            index = jnp.where(last, lax.div(v, 2), index)
+            source = jnp.where(late, far_corner, source)
+            half = jnp.where(late, 1, half)
+            index = jnp.where(late, s - 28, index)
+            job(source, half, index)
+
+        def until(t):
+            total = 0
+            for when, count in ((17, 2), (18, 2), (19, 2), (20, 2), (21, 2), (23, 1), (25, 2), (26, 1),
+                                (29, 2), (30, 2), (31, 2), (32, 3)):
+                total = total + jnp.where(t >= when, count, 0)
+            return total
+
+        @pl.loop(0, SUM_AT + STEPS)
+        def _(t):
+            @pl.when(t < STEPS)
+            def _():
+                for index in range(2):
+                    c_copy(0, slot, 2 * t + index).wait_recv()
+                    c_copy(2 + index, slot, 2 * t + index).start()
+
+                @pl.when(t < FINE // 2 - HEAD)
+                def _():
+                    b_copy(0, row, HEAD + t, True).start()
+                    b_copy(1, row, HEAD + t, True).start()
+                a_wait(other_middle, t)
+                a_copy(2, partner, other_middle, t).start()
+                split_rows(slot, rows_of(t, 2 * b_size), c_all, c_high, c_low)
+
+            @pl.when(t == STEPS)
+            def _():
+                b_wait(x_near, 0, FINE // 2)
+                b_wait(y_near, 0, FINE // 2)
+
+                @pl.loop(0, FINE // 4)
+                def _(step):
+                    b_copy(1, x_near, step).start()
+                    b_copy(0, y_near, FINE // 4 + step).start()
+
+                @pl.loop(0, FINE // 2)
+                def _(step):
+                    b_copy(0, row, FINE // 2 + step, True).start()
+                    b_copy(1, row, FINE // 2 + lax.rem(step + FINE // 4, FINE // 2), True).start()
+                split_b(x_near, 0, 4)
+                split_b(y_near, 0, 4)
+
+            @pl.when((t >= END_AT + PRE) & (t < END_AT + STEPS))
+            def _():
+                a_wait(end, t - END_AT)
+                a_copy(0, other_middle, end, t - END_AT).start()
+                a_copy(2, partner, end, t - END_AT).start()
+
+            @pl.when((t >= FAR_AT) & (t < FAR_AT + STEPS))
+            def _():
+                a_wait(other_end, t - FAR_AT)
+                a_copy(2, partner, other_end, t - FAR_AT).start()
+
+            @pl.when((t >= 2) & (t < STEPS + 2))
+            def _():
+                a_wait(middle + swap, t - 2)
+                a_wait(other_middle + swap, t - 2)
+                for index in range(2):
+                    c_copy(0, 1 - slot, 2 * (t - 2) + index).wait_recv()
+                split_rows(1 - slot, rows_of(t - 2, 2 * b_size), c_all, c_high, c_low)
+
+            @pl.when((t > END_AT) & (t < END_AT + 1 + STEPS))
+            def _():
+                a_wait(end + swap, t - END_AT - 1)
+
+            @pl.when(t == 22)
+            def _():
+                b_wait(far_corner, 0, FINE // 2)
+                split_b(far_corner, 0, 4)
+
+            @pl.when(t == 26)
+            def _():
+                b_wait(x_near, FINE // 2, FINE // 4 * 3)
+                b_wait(y_near, FINE // 4 * 3, FINE)
+
+                @pl.loop(0, FINE // 4)
+                def _(step):
+                    b_copy(1, x_near, FINE // 2 + step).start()
+                    b_copy(0, y_near, FINE // 4 * 3 + step).start()
+
+            @pl.when(t == 29)
+            def _():
+                b_wait(x_near, FINE // 4 * 3, FINE)
+                b_wait(y_near, FINE // 2, FINE // 4 * 3)
+                split_b(x_near, 4, 8)
+                split_b(y_near, 4, 8)
+
+            @pl.when(t >= SUM_AT)
+            def _():
+                step = t - SUM_AT
+                part = rows_of(step, a_size)
+                a_wait(other_end + swap, step)
+                value = None
+                for index in range(4):
+                    piece = term(part, 4 * other_side + index, c_high, c_low, index // 2, index % 2)
+                    value = piece if value is None else value + piece
+                partial[part, :] = value
+
+                @pl.loop(until(t - 1), until(t))
+                def _(s):
+                    sequence(s)
+                p_copy(step).start()
+
+        b_wait(far_corner, FINE // 2, FINE)
+        split_b(far_corner, 4, 8)
+
+        @pl.loop(until(SUM_AT + STEPS), 8 * GROUPS)
+        def _(s):
+            sequence(s)
+
+        for kind in range(3):
+            a_sent(kind, col)
+        a_sent(2, other_middle)
+        a_sent(0, end)
+        a_sent(2, end)
+        a_sent(2, other_end)
+        c_sent(2, b_depth // 2)
+        c_sent(3, b_depth // 2)
+        b_sent(0, row, b_depth)
+        b_sent(1, row, b_depth)
+        b_sent(0, y_near, b_depth // 2)
+        b_sent(1, x_near, b_depth // 2)
+        remote(partial, partial, p_send, p_recv.at[0], {"col": end}).wait_send()
 
 
 def shared_body(left_matrix, right_matrix):
@@ -509,8 +662,8 @@
             pltpu.VMEM((2, b_depth, width), jnp.bfloat16),
             pltpu.VMEM((2, b_depth, width), jnp.bfloat16),
             pltpu.VMEM((height, width), jnp.float32),
-            dma((8, STEPS)), dma((3, 8, STEPS)), dma((4, STEPS)), dma((3, STEPS)),
-            dma((2, STEPS)), dma((2, STEPS)), dma((STEPS,)), dma((STEPS,)), dma((2,)),
+            dma((8, STEPS)), dma((3, 8)), dma((4, FINE)), dma((2, 4)),
+            dma((2, FINE)), dma((4,)), dma((STEPS,)), dma(()), dma((2,)),
         ],
         compiler_params=pltpu.CompilerParams(
             collective_id=1, has_side_effects=True, vmem_limit_bytes=60 * 2**20),

time: 140 us -> 124 us (0.89)
  the two profiles are of different devices: /device:TPU:17 before, /device:TPU:0 now
where the time goes in v1:
time: 124 us
  Pallas kernels  121 us (98%)
  local copies, waits for them, and re-layouts  3.08 us (2%)
    pallas_call x1, Pallas kernels, shared_body(): pl.pallas_call(shared_kernel, out_shape=jax.ShapeDtypeStruct((height, wid...  121 us
    unnamed x1, local copies, waits for them, and re-layouts  3.08 us

profile of v1, /device:TPU:0, one launch (start us, length us, event | category | flops | bytes accessed | tf_op | source)
XLA Modules:
  0.0 123.7 jit_solution(7892407987532179668)
XLA Ops:
  0.0 120.6 %shard_map.28 = f32[1024,512]{1,0:T(8,128)} custom-call(f32[1024,512]{1,0:T(8,128)} %a_in.1, f32[1024,512]{1,0:T(8,128)} %b_in.1), custom_call_target="tpu_custom_call" | custom-call | tf_op jit(solution)/shard_map/pallas_call | solution.py:651
  120.6 3.1 %copy.4 = f32[1024,512]{1,0:T(8,128)} copy(f32[1024,512]{1,0:T(8,128)} %shard_map.28) | data formatting | bytes 4194304

commit v2 on v1

--- a/solution.py
+++ b/solution.py
@@ -198,7 +198,7 @@
     return pl.pallas_call(
         functools.partial(kernel, rows, cols),
         out_shape=jax.ShapeDtypeStruct((height, width), jnp.float32),
-        in_specs=[pl.BlockSpec(memory_space=pl.ANY)] * 2,
+        in_specs=[pl.BlockSpec(memory_space=pltpu.HBM)] * 2,
         out_specs=pl.BlockSpec(memory_space=pltpu.VMEM),
         scratch_shapes=[
             pltpu.VMEM((cols, height, a_depth), jnp.float32),
@@ -218,10 +218,17 @@
 
 STEPS = 16
 FINE = 32
-HEAD = 4
+HEAD = 8
 PRE = 1
+MORE = 1
 GROUPS = 4
-END_AT = 13
+LACK = 2
+LENT = FINE // 2 - LACK
+LENT_AT = 3
+LACK_AT = 5
+RELAY_AT = 14
+LAST_AT = 26
+END_AT = 14
 FAR_AT = 16
 SUM_AT = 17
 LANDED_AT = 20
@@ -303,6 +310,9 @@
         remote(c_all.at[0, part], c_all.at[0, part], c_send.at[kind], c_recv.at[0, 0],
                {"row": x_near}).wait_send()
 
+    def lent(step, held):
+        return step + jnp.where(held & (step < 2 * LACK), 0, 2 * LACK)
+
     def p_copy(step):
         part = rows_of(step, a_size)
         return remote(partial.at[part], partial.at[part], p_send, p_recv.at[step], {"col": end})
@@ -365,10 +375,10 @@
 
         @pl.when(donor)
         def _():
-            @pl.loop(0, FINE)
+            @pl.loop(0, 2 * LENT)
             def _(step):
-                c_copy(1, x, step, True).start()
-                c_copy(0, x, step, True).start()
+                c_copy(1, x, lent(step, True), True).start()
+                c_copy(0, x, lent(step, False), True).start()
 
             @pl.loop(PRE, STEPS)
             def _(step):
@@ -381,6 +391,9 @@
                 b_copy(0, row, step, True).start()
                 b_copy(1, row, step, True).start()
 
+            for step in range(PRE, PRE + MORE):
+                a_copy(0, middle, col, step, True).start()
+
         @pl.loop(0, STEPS)
         def _(step):
             a_copy(2, partner, col, step, True).start()
@@ -390,17 +403,21 @@
 
         @pl.loop(0, LANDED_AT + STEPS)
         def _(t):
-            @pl.when(keeper & (t < STEPS))
+            @pl.when(keeper & (t < LENT))
             def _():
                 for index in range(2):
-                    c_copy(0, 1 - x, 2 * t + index).wait_recv()
-                    c_copy(0, 1 - x, 2 * t + index).start()
-
-            @pl.when(keeper & (t == STEPS))
-            def _():
-                @pl.loop(PRE, STEPS)
+                    chunk = lent(2 * t + index, True)
+                    c_copy(0, 1 - x, chunk).wait_recv()
+                    c_copy(0, 1 - x, chunk).start()
+
+            @pl.when(keeper & (t == LENT))
+            def _():
+                @pl.loop(PRE + MORE, STEPS)
                 def _(step):
                     a_copy(0, middle, col, step, True).start()
+
+            @pl.when(keeper & (t == STEPS + 1))
+            def _():
                 b_wait(x_near, 0, FINE)
 
             @pl.when(donor & (t < STEPS))
@@ -460,13 +477,13 @@
 
         @pl.when(donor)
         def _():
-            c_sent(0, b_depth)
-            c_sent(1, b_depth)
+            c_sent(0, 2 * LENT * b_size)
+            c_sent(1, 2 * LENT * b_size)
             b_sent(0, y_near, b_depth)
 
         @pl.when(keeper)
         def _():
-            c_sent(0, b_depth)
+            c_sent(0, 2 * LENT * b_size)
             b_sent(0, row, b_depth)
             b_sent(1, row, b_depth)
         a_sent(0, col)
@@ -477,6 +494,25 @@
     def _():
         inner = (row == 1) | (row == 2)
         slot = lax.rem(x + jnp.where(keeper, 1, 0), 2)
+        mine = jnp.where(keeper, 2 * LACK, 0)
+        theirs = 2 * LACK - mine
+
+        def within(chunk, start):
+            return (chunk >= start) & (chunk < start + 2 * LACK)
+
+        def c_split(which, step):
+            split_rows(which, rows_of(step, 2 * b_size), c_all, c_high, c_low)
+
+        def c_landed(chunk):
+            c_copy(0, 1 - slot, chunk).wait_recv()
+
+            @pl.when(within(chunk, mine) & (lax.rem(chunk, 2) == 0))
+            def _():
+                c_copy(2, 1 - slot, chunk).start()
+
+            @pl.when(within(chunk, theirs) & (lax.rem(chunk, 2) == 1))
+            def _():
+                c_copy(3, 1 - slot, chunk).start()
 
         @pl.loop(0, STEPS)
         def _(step):
@@ -523,31 +559,44 @@
 
         def until(t):
             total = 0
-            for when, count in ((17, 2), (18, 2), (19, 2), (20, 2), (21, 2), (23, 1), (25, 2), (26, 1),
-                                (29, 2), (30, 2), (31, 2), (32, 3)):
+            for when, count in ((17, 2), (18, 2), (19, 2), (20, 2), (21, 2), (23, 1), (24, 2), (25, 1),
+                                (28, 2), (29, 2), (30, 2), (31, 2), (32, 1)):
                 total = total + jnp.where(t >= when, count, 0)
             return total
 
         @pl.loop(0, SUM_AT + STEPS)
         def _(t):
+            @pl.when(t < LENT)
+            def _():
+                for index in range(2):
+                    chunk = lent(2 * t + index, keeper)
+                    c_copy(0, slot, chunk).wait_recv()
+                    both = within(chunk, theirs)
+
+                    @pl.when(both | (lax.rem(chunk, 2) == 0))
+                    def _():
+                        c_copy(2, slot, chunk).start()
+
+                    @pl.when(both | (lax.rem(chunk, 2) == 1))
+                    def _():
+                        c_copy(3, slot, chunk).start()
+                c_split(slot, lax.div(lent(2 * t, keeper), 2))
+
+            @pl.when(t < (FINE // 2 - HEAD) // 2)
+            def _():
+                for index in range(2):
+                    b_copy(0, row, HEAD + 2 * t + index, True).start()
+                    b_copy(1, row, HEAD + 2 * t + index, True).start()
+
             @pl.when(t < STEPS)
             def _():
-                for index in range(2):
-                    c_copy(0, slot, 2 * t + index).wait_recv()
-                    c_copy(2 + index, slot, 2 * t + index).start()
-
-                @pl.when(t < FINE // 2 - HEAD)
-                def _():
-                    b_copy(0, row, HEAD + t, True).start()
-                    b_copy(1, row, HEAD + t, True).start()
                 a_wait(other_middle, t)
                 a_copy(2, partner, other_middle, t).start()
-                split_rows(slot, rows_of(t, 2 * b_size), c_all, c_high, c_low)
-
-            @pl.when(t == STEPS)
-            def _():
-                b_wait(x_near, 0, FINE // 2)
-                b_wait(y_near, 0, FINE // 2)
+
+            @pl.when(t == RELAY_AT)
+            def _():
+                b_wait(x_near, 0, FINE // 4)
+                b_wait(y_near, FINE // 4, FINE // 2)
 
                 @pl.loop(0, FINE // 4)
                 def _(step):
@@ -558,6 +607,11 @@
                 def _(step):
                     b_copy(0, row, FINE // 2 + step, True).start()
                     b_copy(1, row, FINE // 2 + lax.rem(step + FINE // 4, FINE // 2), True).start()
+
+            @pl.when(t == RELAY_AT + 2)
+            def _():
+                b_wait(x_near, FINE // 4, FINE // 2)
+                b_wait(y_near, 0, FINE // 4)
                 split_b(x_near, 0, 4)
                 split_b(y_near, 0, 4)
 
@@ -576,20 +630,37 @@
             def _():
                 a_wait(middle + swap, t - 2)
                 a_wait(other_middle + swap, t - 2)
-                for index in range(2):
-                    c_copy(0, 1 - slot, 2 * (t - 2) + index).wait_recv()
-                split_rows(1 - slot, rows_of(t - 2, 2 * b_size), c_all, c_high, c_low)
+
+            @pl.when((t >= LENT_AT) & (t < LENT_AT + LENT))
+            def _():
+                u = t - LENT_AT
+
+                @pl.when(u < LACK)
+                def _():
+                    c_landed(2 * u)
+                    c_landed(2 * u + 1)
+                    c_split(1 - slot, u)
+                c_landed(2 * LACK + 2 * u)
+                c_landed(2 * LACK + 2 * u + 1)
+                c_split(1 - slot, LACK + u)
+
+            @pl.when((t >= LACK_AT) & (t < LACK_AT + LACK))
+            def _():
+                chunk = mine + 2 * (t - LACK_AT)
+                c_copy(0, slot, chunk).wait_recv()
+                c_copy(0, slot, chunk + 1).wait_recv()
+                c_split(slot, lax.div(chunk, 2))
 
             @pl.when((t > END_AT) & (t < END_AT + 1 + STEPS))
             def _():
                 a_wait(end + swap, t - END_AT - 1)
 
-            @pl.when(t == 22)
+            @pl.when(t == 21)
             def _():
                 b_wait(far_corner, 0, FINE // 2)
                 split_b(far_corner, 0, 4)
 
-            @pl.when(t == 26)
+            @pl.when(t == LAST_AT)
             def _():
                 b_wait(x_near, FINE // 2, FINE // 4 * 3)
                 b_wait(y_near, FINE // 4 * 3, FINE)
@@ -599,7 +670,7 @@
                     b_copy(1, x_near, FINE // 2 + step).start()
                     b_copy(0, y_near, FINE // 4 * 3 + step).start()
 
-            @pl.when(t == 29)
+            @pl.when(t == LAST_AT + 3)
             def _():
                 b_wait(x_near, FINE // 4 * 3, FINE)
                 b_wait(y_near, FINE // 2, FINE // 4 * 3)
@@ -609,18 +680,22 @@
             @pl.when(t >= SUM_AT)
             def _():
                 step = t - SUM_AT
-                part = rows_of(step, a_size)
                 a_wait(other_end + swap, step)
-                value = None
-                for index in range(4):
-                    piece = term(part, 4 * other_side + index, c_high, c_low, index // 2, index % 2)
-                    value = piece if value is None else value + piece
-                partial[part, :] = value
+
+                @pl.when(lax.rem(step, 2) == 1)
+                def _():
+                    part = rows_of(lax.div(step, 2), 2 * a_size)
+                    value = None
+                    for index in range(4):
+                        piece = term(part, 4 * other_side + index, c_high, c_low, index // 2, index % 2)
+                        value = piece if value is None else value + piece
+                    partial[part, :] = value
+                    p_copy(step - 1).start()
+                    p_copy(step).start()
 
                 @pl.loop(until(t - 1), until(t))
                 def _(s):
                     sequence(s)
-                p_copy(step).start()
 
         b_wait(far_corner, FINE // 2, FINE)
         split_b(far_corner, 4, 8)
@@ -635,8 +710,8 @@
         a_sent(0, end)
         a_sent(2, end)
         a_sent(2, other_end)
-        c_sent(2, b_depth // 2)
-        c_sent(3, b_depth // 2)
+        c_sent(2, (FINE // 2 + LACK) * b_size)
+        c_sent(3, (FINE // 2 + LACK) * b_size)
         b_sent(0, row, b_depth)
         b_sent(1, row, b_depth)
         b_sent(0, y_near, b_depth // 2)
@@ -651,7 +726,7 @@
     return pl.pallas_call(
         shared_kernel,
         out_shape=jax.ShapeDtypeStruct((height, width), jnp.float32),
-        in_specs=[pl.BlockSpec(memory_space=pl.ANY)] * 2,
+        in_specs=[pl.BlockSpec(memory_space=pltpu.HBM)] * 2,
         out_specs=pl.BlockSpec(memory_space=pltpu.VMEM),
         scratch_shapes=[
             pltpu.VMEM((8, height, a_depth), jnp.float32),
@@ -666,7 +741,7 @@
             dma((2, FINE)), dma((4,)), dma((STEPS,)), dma(()), dma((2,)),
         ],
         compiler_params=pltpu.CompilerParams(
-            collective_id=1, has_side_effects=True, vmem_limit_bytes=60 * 2**20),
+            collective_id=1, has_side_effects=True, vmem_limit_bytes=48 * 2**20),
     )(left_matrix, right_matrix)
 
 

time: 124 us -> 114 us (0.919)
  Pallas kernels: 121 us -> 111 us
    pallas_call x1, Pallas kernels: 121 us -> 111 us  [shared_body(): pl.pallas_call(shared_kernel, out_shape=jax.ShapeDtypeStruct((height, wid...]
    unnamed x1 -> x3, local copies, waits for them, and re-layouts: 3.08 us -> 2.91 us
where the time goes in v2:
time: 114 us
  Pallas kernels  111 us (97%)
  local copies, waits for them, and re-layouts  2.91 us (3%)
    pallas_call x1, Pallas kernels, shared_body(): pl.pallas_call(shared_kernel, out_shape=jax.ShapeDtypeStruct((height, wid...  111 us
    unnamed x3, local copies, waits for them, and re-layouts  2.91 us

profile of v2, /device:TPU:0, one launch (start us, length us, event | category | flops | bytes accessed | tf_op | source)
XLA Modules:
  0.0 113.9 jit_solution(8408610571233701584)
XLA Ops:
  0.0 0.0 copy-start
  0.0 1.6 %copy-done = f32[1024,512]{1,0:T(8,128)S(1)} copy-done((f32[1024,512]{1,0:T(8,128)S(1)}, f32[1024,512]{1,0:T(8,128)}, u32[]{:S(2)}) %copy-start) | copy-done | bytes 2097176
  1.6 111.0 %shard_map.28 = f32[1024,512]{1,0:T(8,128)S(1)} custom-call(f32[1024,512]{1,0:T(8,128)S(1)} %copy-done, f32[1024,512]{1,0:T(8,128)} %b_in.1), custom_call_target="tpu_custom_call" | custom-call | tf_op jit(solution)/shard_map/pallas_call | solution.py:726
  112.6 1.3 %copy.4 = f32[1024,512]{1,0:T(8,128)} copy(f32[1024,512]{1,0:T(8,128)S(1)} %shard_map.28) | data formatting | bytes 4194304
Async XLA Ops:
  0.0 1.6 %copy-start = (f32[1024,512]{1,0:T(8,128)S(1)}, f32[1024,512]{1,0:T(8,128)}, u32[]{:S(2)}) copy-start(f32[1024,512]{1,0:T(8,128)} %a_in.1) | copy-start | bytes 6291460

commit v3 on v2

--- a/solution.py
+++ b/solution.py
@@ -226,11 +226,14 @@
 LENT = FINE // 2 - LACK
 LENT_AT = 3
 LACK_AT = 5
-RELAY_AT = 14
-LAST_AT = 26
+OWN_AT = 14
+NEAR_AT = 16
+RELAY_AT = 21
+LAST_AT = 24
+FAR_B_AT = 28
 END_AT = 14
 FAR_AT = 16
-SUM_AT = 17
+SUM_AT = 16
 LANDED_AT = 20
 
 
@@ -336,8 +339,8 @@
         right_low = low_all[source, depth, :]
         return (dot(low, right_high) + dot(high, right_low)) + dot(high, right_high)
 
-    def job(source, half, index):
-        part = rows_of(index, group)
+    def job(source, half, index, size=group):
+        part = rows_of(index, size)
         out[part, :] += term(part, 2 * source + half, b_high, b_low, source, half)
 
     barrier = pltpu.get_barrier_semaphore()
@@ -534,33 +537,29 @@
             a_copy(2, partner, end, step).start()
 
         def sequence(s):
-            late = s >= 28
-            q = jnp.where(s >= 23, s - 14, s - 8)
-            g, w = lax.div(q, 3), lax.rem(q, 3)
-            last = (s >= 17) & (s < 23) | (s == 26) | (s == 27)
-            v = jnp.where(s >= 26, s - 20, s - 17)
-            near = lambda p: jnp.where(p == 0, x_near, y_near)
+            def near(p):
+                return jnp.where(p == 0, x_near, y_near)
+
+            def choose(test, new, old):
+                return tuple(jnp.where(test, a, b) for a, b in zip(new, old))
+
             u = lax.rem(s, 8)
-            source = jnp.where(inner, row, near(lax.div(u, GROUPS)))
-            half = jnp.where(inner, lax.div(u, GROUPS), 0)
-            index = lax.rem(u, GROUPS)
-            mid = (s >= 8) & (s < 28)
-            pair = mid & (w < 2)
-            source = jnp.where(mid, jnp.where(w < 2, jnp.where(inner, near(w), row), far_corner), source)
-            half = jnp.where(mid, jnp.where(pair & ~inner, w, 0), half)
-            index = jnp.where(mid, g, index)
-            source = jnp.where(last, near(lax.rem(v, 2)), source)
-            half = jnp.where(last, 1, half)
-            index = jnp.where(last, lax.div(v, 2), index)
-            source = jnp.where(late, far_corner, source)
-            half = jnp.where(late, 1, half)
-            index = jnp.where(late, s - 28, index)
-            job(source, half, index)
+            block, index = lax.div(u, GROUPS), lax.rem(u, GROUPS)
+            value = choose(inner, (row, block, index), (near(block), 0, index))
+            w = lax.rem(s, 2)
+            g = jnp.where(s < 10, 0, jnp.where(s < 12, 1, jnp.where(s < 14, 0, jnp.where(s < 16, 1,
+                jnp.where(s < 20, 2, 3)))))
+            upper = ((s >= 12) & (s < 16)) | ((s >= 18) & (s < 20)) | (s >= 26)
+            second = choose(inner, (near(w), 0, g), (row, w, g))
+            second = choose(upper, (near(w), 1, g), second)
+            value = choose(s >= 8, second, value)
+            value = choose((s >= 20) & (s < 24), (far_corner, 0, s - 20), value)
+            job(*value)
 
         def until(t):
             total = 0
-            for when, count in ((17, 2), (18, 2), (19, 2), (20, 2), (21, 2), (23, 1), (24, 2), (25, 1),
-                                (28, 2), (29, 2), (30, 2), (31, 2), (32, 1)):
+            for when, count in ((17, 2), (18, 2), (19, 1), (20, 2), (21, 2), (22, 1), (24, 1), (25, 2),
+                                (26, 2), (27, 1), (28, 2), (29, 2), (30, 2), (31, 1)):
                 total = total + jnp.where(t >= when, count, 0)
             return total
 
@@ -593,27 +592,46 @@
                 a_wait(other_middle, t)
                 a_copy(2, partner, other_middle, t).start()
 
-            @pl.when(t == RELAY_AT)
-            def _():
-                b_wait(x_near, 0, FINE // 4)
-                b_wait(y_near, FINE // 4, FINE // 2)
+            @pl.when(t == OWN_AT)
+            def _():
+                @pl.loop(0, FINE // 2)
+                def _(step):
+                    b_copy(0, row, FINE // 2 + step, True).start()
+                    b_copy(1, row, FINE // 2 + lax.rem(step + FINE // 4, FINE // 2), True).start()
+
+            @pl.when(t == NEAR_AT)
+            def _():
+                b_wait(x_near, 0, FINE // 2)
+                b_wait(y_near, 0, FINE // 2)
 
                 @pl.loop(0, FINE // 4)
                 def _(step):
                     b_copy(1, x_near, step).start()
                     b_copy(0, y_near, FINE // 4 + step).start()
-
-                @pl.loop(0, FINE // 2)
-                def _(step):
-                    b_copy(0, row, FINE // 2 + step, True).start()
-                    b_copy(1, row, FINE // 2 + lax.rem(step + FINE // 4, FINE // 2), True).start()
-
-            @pl.when(t == RELAY_AT + 2)
-            def _():
-                b_wait(x_near, FINE // 4, FINE // 2)
-                b_wait(y_near, 0, FINE // 4)
                 split_b(x_near, 0, 4)
                 split_b(y_near, 0, 4)
+
+            @pl.when(t == RELAY_AT)
+            def _():
+                b_wait(x_near, FINE // 2, FINE // 4 * 3)
+                b_wait(y_near, FINE // 4 * 3, FINE)
+
+                @pl.loop(0, FINE // 4)
+                def _(step):
+                    b_copy(1, x_near, FINE // 2 + step).start()
+                    b_copy(0, y_near, FINE // 4 * 3 + step).start()
+
+            @pl.when(t == LAST_AT)
+            def _():
+                b_wait(x_near, FINE // 4 * 3, FINE)
+                b_wait(y_near, FINE // 2, FINE // 4 * 3)
+                split_b(x_near, 4, 8)
+                split_b(y_near, 4, 8)
+
+            @pl.when(t == FAR_B_AT)
+            def _():
+                b_wait(far_corner, 0, FINE // 2)
+                split_b(far_corner, 0, 4)
 
             @pl.when((t >= END_AT + PRE) & (t < END_AT + STEPS))
             def _():
@@ -655,54 +673,37 @@
             def _():
                 a_wait(end + swap, t - END_AT - 1)
 
-            @pl.when(t == 21)
-            def _():
-                b_wait(far_corner, 0, FINE // 2)
-                split_b(far_corner, 0, 4)
-
-            @pl.when(t == LAST_AT)
-            def _():
-                b_wait(x_near, FINE // 2, FINE // 4 * 3)
-                b_wait(y_near, FINE // 4 * 3, FINE)
-
-                @pl.loop(0, FINE // 4)
-                def _(step):
-                    b_copy(1, x_near, FINE // 2 + step).start()
-                    b_copy(0, y_near, FINE // 4 * 3 + step).start()
-
-            @pl.when(t == LAST_AT + 3)
-            def _():
-                b_wait(x_near, FINE // 4 * 3, FINE)
-                b_wait(y_near, FINE // 2, FINE // 4 * 3)
-                split_b(x_near, 4, 8)
-                split_b(y_near, 4, 8)
-
-            @pl.when(t >= SUM_AT)
-            def _():
-                step = t - SUM_AT
-                a_wait(other_end + swap, step)
-
-                @pl.when(lax.rem(step, 2) == 1)
-                def _():
-                    part = rows_of(lax.div(step, 2), 2 * a_size)
-                    value = None
-                    for index in range(4):
-                        piece = term(part, 4 * other_side + index, c_high, c_low, index // 2, index % 2)
-                        value = piece if value is None else value + piece
-                    partial[part, :] = value
-                    p_copy(step - 1).start()
-                    p_copy(step).start()
-
+            @pl.when((t == SUM_AT) | (t == SUM_AT + 3) | (t == SUM_AT + 7) | (t == SUM_AT + 11))
+            def _():
+                part = rows_of(lax.div(t - SUM_AT + 1, 4), group)
+                partial[part, :] = (term(part, 2 * (2 - side), c_high, c_low, side, 0)
+                                    + term(part, 2 * (2 - side) + 1, c_high, c_low, side, 1))
+
+            @pl.when(t > SUM_AT)
+            def _():
                 @pl.loop(until(t - 1), until(t))
                 def _(s):
                     sequence(s)
 
+            @pl.when(t >= SUM_AT)
+            def _():
+                step = t - SUM_AT
+                a_wait(other_end + swap, step)
+                part = rows_of(step, a_size)
+                partial[part, :] += (term(part, 6 - 6 * side, c_high, c_low, other_side, 0)
+                                     + term(part, 7 - 6 * side, c_high, c_low, other_side, 1))
+                p_copy(step).start()
+
+        @pl.loop(until(SUM_AT + STEPS), 7 * GROUPS)
+        def _(s):
+            sequence(s)
+
         b_wait(far_corner, FINE // 2, FINE)
         split_b(far_corner, 4, 8)
 
-        @pl.loop(until(SUM_AT + STEPS), 8 * GROUPS)
-        def _(s):
-            sequence(s)
+        @pl.loop(0, 2)
+        def _(index):
+            job(far_corner, 1, index, 2 * group)
 
         for kind in range(3):
             a_sent(kind, col)

time: 114 us -> 111 us (0.974)
  Pallas kernels: 111 us -> 108 us
    pallas_call x1, Pallas kernels: 111 us -> 108 us  [shared_body(): pl.pallas_call(shared_kernel, out_shape=jax.ShapeDtypeStruct((height, wid...]
where the time goes in v3:
time: 111 us
  Pallas kernels  108 us (97%)
  local copies, waits for them, and re-layouts  2.91 us (3%)
    pallas_call x1, Pallas kernels, shared_body(): pl.pallas_call(shared_kernel, out_shape=jax.ShapeDtypeStruct((height, wid...  108 us
    unnamed x3, local copies, waits for them, and re-layouts  2.91 us

profile of v3, /device:TPU:0, one launch (start us, length us, event | category | flops | bytes accessed | tf_op | source)
XLA Modules:
  0.0 110.9 jit_solution(18268595800159965263)
XLA Ops:
  0.0 0.0 copy-start
  0.0 1.6 %copy-done = f32[1024,512]{1,0:T(8,128)S(1)} copy-done((f32[1024,512]{1,0:T(8,128)S(1)}, f32[1024,512]{1,0:T(8,128)}, u32[]{:S(2)}) %copy-start) | copy-done | bytes 2097176
  1.6 108.0 %shard_map.28 = f32[1024,512]{1,0:T(8,128)S(1)} custom-call(f32[1024,512]{1,0:T(8,128)S(1)} %copy-done, f32[1024,512]{1,0:T(8,128)} %b_in.1), custom_call_target="tpu_custom_call" | custom-call | tf_op jit(solution)/shard_map/pallas_call | solution.py:727
  109.6 1.3 %copy.4 = f32[1024,512]{1,0:T(8,128)} copy(f32[1024,512]{1,0:T(8,128)S(1)} %shard_map.28) | data formatting | bytes 4194304
Async XLA Ops:
  0.0 1.6 %copy-start = (f32[1024,512]{1,0:T(8,128)S(1)}, f32[1024,512]{1,0:T(8,128)}, u32[]{:S(2)}) copy-start(f32[1024,512]{1,0:T(8,128)} %a_in.1) | copy-start | bytes 6291460

commit v4 on v3

--- a/solution.py
+++ b/solution.py
@@ -328,7 +328,7 @@
     def split_b(source, first, last):
         @pl.loop(first, last)
         def _(index):
-            split_rows(source, rows_of(index, 128), b_all, b_high, b_low)
+            split_rows(source, rows_of(index, 4 * b_size), b_all, b_high, b_low)
 
     dot = functools.partial(jnp.dot, preferred_element_type=jnp.float32)
 

time: 111 us -> 111 us (level)
  no operation moved by 1% of the time
where the time goes in v4:
time: 111 us
  Pallas kernels  108 us (97%)
  local copies, waits for them, and re-layouts  2.91 us (3%)
    pallas_call x1, Pallas kernels, shared_body(): pl.pallas_call(shared_kernel, out_shape=jax.ShapeDtypeStruct((height, wid...  108 us
    unnamed x3, local copies, waits for them, and re-layouts  2.91 us

profile of v4, /device:TPU:0, one launch (start us, length us, event | category | flops | bytes accessed | tf_op | source)
XLA Modules:
  0.0 110.9 jit_solution(18268595800159965263)
XLA Ops:
  0.0 0.0 copy-start
  0.0 1.6 %copy-done = f32[1024,512]{1,0:T(8,128)S(1)} copy-done((f32[1024,512]{1,0:T(8,128)S(1)}, f32[1024,512]{1,0:T(8,128)}, u32[]{:S(2)}) %copy-start) | copy-done | bytes 2097176
  1.6 108.0 %shard_map.28 = f32[1024,512]{1,0:T(8,128)S(1)} custom-call(f32[1024,512]{1,0:T(8,128)S(1)} %copy-done, f32[1024,512]{1,0:T(8,128)} %b_in.1), custom_call_target="tpu_custom_call" | custom-call | tf_op jit(solution)/shard_map/pallas_call | solution.py:727
  109.6 1.3 %copy.4 = f32[1024,512]{1,0:T(8,128)} copy(f32[1024,512]{1,0:T(8,128)S(1)} %shard_map.28) | data formatting | bytes 4194304
Async XLA Ops:
  0.0 1.6 %copy-start = (f32[1024,512]{1,0:T(8,128)S(1)}, f32[1024,512]{1,0:T(8,128)}, u32[]{:S(2)}) copy-start(f32[1024,512]{1,0:T(8,128)} %a_in.1) | copy-start | bytes 6291460
